TPU v7x, 32 devices: a whole 2x2x4 slice. The times are simulated.
32 devices in a mesh: group: 2 (over y), ctx: 4 (over z), head: 4 (over x, core).
Axes of the slice: x: 2, y: 2, z: 4, core: 2. Of those that a mesh axis runs over, the one named last changes fastest.
Arguments:
- query_nope: bfloat16 [512, 8192], P(('group', 'ctx'), 'head'), parts along dimension 0, may hold values from -6 to 6
- query_rope: bfloat16 [512, 4096], P(('group', 'ctx'), 'head'), parts along dimension 0, may hold values from -16 to 16
- kv_latent: bfloat16 [512, 512], P(('group', 'ctx'), 'head'), parts along dimension 0, may hold values from -1300 to 1300
- key_rope: bfloat16 [512, 64], P(('group', 'ctx')), parts along dimension 0, may hold values from -16 to 16
- latent_gain: float32 [512], replicated, may hold values from 0.1 to 1.9
- w_key: bfloat16 [512, 8192], P(None, 'head'), may hold values from -0.25 to 0.25
- w_value: bfloat16 [512, 8192], P(None, 'head'), may hold values from -0.25 to 0.25
- block_order: int32 [16], P('group'), parts along dimension 0, may hold values from 0 to 7, as said below
Outputs:
- attention_out: bfloat16 [512, 8192], P(('group', 'ctx'), 'head'), parts along dimension 0
There are 2 independent parts, one for each index of `group`. A program takes and returns all parts, laid end to end along the dimension named above; an argument that names none is the same for every part. Nothing has to cross between parts.
Inputs may be any that keep to these rules, and one draw needn't show every extreme that they name: `block_order`: A permutation of 0 to 7. Entries 2 c and 2 c + 1, for each c < 4, add up to 7.
All inputs are finite; a program needn't handle non-finite values.
Results may differ from a plain program's by a relative error of at most 0.0081.
Values may be sent and summed in bfloat16 or wider, within the bound.
A program may use at most 64 MiB of HBM per device.

v0:
```python
from functools import partial
import math
import jax
import jax.numpy as jnp
from jax import lax
from jax.sharding import PartitionSpec as P

ROPE = 64
NOPE = 128
VALUE_DIM = 128
EPSILON = 1e-06
NEGATIVE = -1e30


def rope_angle(positions, width):
    half_width = width // 2
    frequency = jnp.exp(-jnp.log(10000.0) * jnp.arange(half_width, dtype=jnp.float32) / half_width)
    return positions.astype(jnp.float32)[:, None] * frequency[None, :]


def rotate_pairs(values, angle):
    half_width = values.shape[-1] // 2
    first_half = values[..., :half_width]
    second = values[..., half_width:]
    cosine = jnp.cos(angle)
    sine_part = jnp.sin(angle)
    return jnp.concatenate(
        [first_half * cosine - second * sine_part, second * cosine + first_half * sine_part], -1
    )


def block_positions(begin_row, row_count, table, block_rows):
    row_ids = begin_row + jnp.arange(row_count, dtype=jnp.int32)
    blocks = row_ids // block_rows
    slot_ids = jnp.arange(table.shape[0], dtype=jnp.int32)
    looked = jnp.sum(jnp.where(blocks[:, None] == slot_ids[None, :], table[None, :], 0), axis=1)
    return looked * block_rows + row_ids % block_rows


def block_length(row_count, shard_rows):
    best_rows = shard_rows
    for factor in range(1, row_count // shard_rows + 1):
        if row_count // shard_rows % factor == 0 and shard_rows * factor <= max(512, shard_rows):
            best_rows = shard_rows * factor
    return best_rows


def attend_block(
    carried,
    query_latent,
    query_rotated,
    query_place,
    key_latent,
    key_rotated,
    key_place,
    score_scale,
):
    running_max, running_total, summed = carried
    contract = (((1,), (1,)), ((), ()))
    scores = lax.dot_general(query_latent, key_latent, contract, preferred_element_type=jnp.float32)
    scores = (
        scores
        + lax.dot_general(query_rotated, key_rotated, contract, preferred_element_type=jnp.float32)
    ) * score_scale
    visible = key_place[None, :] <= query_place[:, None]
    scores = jnp.where(visible, scores, NEGATIVE)
    new_max = jnp.maximum(running_max, jnp.max(scores, axis=1))
    exps = jnp.where(visible, jnp.exp(scores - new_max[:, None]), 0.0)
    shrink = jnp.exp(running_max - new_max)
    running_total = running_total * shrink + jnp.sum(exps, axis=1)
    summed = summed * shrink[:, None] + jnp.dot(
        exps.astype(jnp.bfloat16), key_latent, preferred_element_type=jnp.float32
    )
    return (new_max, running_total, summed)


def per_device(
    query_nope, query_rope, kv_latent, key_rope, latent_gain, w_key, w_value, block_order
):
    tokens_here = query_nope.shape[0]
    heads_here = w_key.shape[1] // NOPE
    latent_width = w_key.shape[0]
    block_rows = tokens_here // 2
    score_scale = 1.0 / math.sqrt(NOPE + ROPE)
    first_row = lax.axis_index("ctx") * tokens_here
    query_place = block_positions(first_row, tokens_here, block_order, block_rows)
    query_angle = rope_angle(query_place, ROPE)
    query_rotated = rotate_pairs(
        query_rope.astype(jnp.float32).reshape(tokens_here, heads_here, ROPE),
        query_angle[:, None, :],
    )
    query_rotated = query_rotated.astype(jnp.bfloat16).reshape(tokens_here * heads_here, ROPE)
    absorbed = jnp.einsum(
        "thd,lhd->thl",
        query_nope.reshape(tokens_here, heads_here, NOPE),
        w_key.reshape(latent_width, heads_here, NOPE),
        preferred_element_type=jnp.float32,
    )
    absorbed = absorbed.astype(jnp.bfloat16).reshape(tokens_here * heads_here, latent_width)
    row_place = jnp.repeat(query_place, heads_here)
    groups = ((absorbed, query_rotated, row_place),)
    initial = tuple(
        (
            (
                jnp.full((member[0].shape[0],), NEGATIVE, jnp.float32),
                jnp.zeros((member[0].shape[0],), jnp.float32),
                jnp.zeros((member[0].shape[0], latent_width), jnp.float32),
            )
            for member in groups
        )
    )
    columns = kv_latent.shape[1]
    column_part = kv_latent.astype(jnp.float32)
    square = lax.psum(jnp.sum(column_part * column_part, axis=1), "head")
    gain_part = lax.dynamic_slice_in_dim(latent_gain, lax.axis_index("head") * columns, columns, 0)
    scaled = (
        column_part * lax.rsqrt(square / latent_width + EPSILON)[:, None] * gain_part[None, :]
    ).astype(jnp.bfloat16)
    normed = lax.all_gather(scaled, "head", axis=1, tiled=True)
    key_rotated = rotate_pairs(key_rope.astype(jnp.float32), query_angle).astype(jnp.bfloat16)
    key_latent = lax.all_gather(normed, "ctx", axis=0, tiled=True)
    make_key_rotated = lax.all_gather(key_rotated, "ctx", axis=0, tiled=True)
    row_count = key_latent.shape[0]
    length = block_length(row_count, tokens_here)
    block_count = row_count // length
    latent_blocks = key_latent.reshape(block_count, length, latent_width)
    rotated_blocks = make_key_rotated.reshape(block_count, length, ROPE)
    block_starts = length * jnp.arange(block_count, dtype=jnp.int32)

    def one_block(state_now, operands):
        latent_block, rotated_block, first_key = operands
        key_place = block_positions(first_key, length, block_order, block_rows)
        updated = []
        for member, member_state in zip(groups, state_now):
            advance = partial(
                attend_block,
                query_latent=member[0],
                query_rotated=member[1],
                query_place=member[2],
                key_latent=latent_block,
                key_rotated=rotated_block,
                key_place=key_place,
                score_scale=score_scale,
            )
            updated.append(advance(member_state))
        return (tuple(updated), None)

    result, unused = lax.scan(one_block, initial, (latent_blocks, rotated_blocks, block_starts))
    mixed = jnp.concatenate(
        [
            (member_state[2] / member_state[1][:, None]).astype(jnp.bfloat16)
            for member_state in result
        ],
        0,
    )
    mixed = mixed.reshape(tokens_here, heads_here, latent_width)
    output = jnp.einsum(
        "thl,lhe->the",
        mixed,
        w_value.reshape(latent_width, heads_here, VALUE_DIM),
        preferred_element_type=jnp.float32,
    )
    return output.astype(jnp.bfloat16).reshape(tokens_here, heads_here * VALUE_DIM)


def solution(mesh):
    return jax.shard_map(
        per_device,
        mesh=mesh,
        in_specs=(
            P(("group", "ctx"), "head"),
            P(("group", "ctx"), "head"),
            P(("group", "ctx"), "head"),
            P(("group", "ctx"), None),
            P(),
            P(None, "head"),
            P(None, "head"),
            P("group"),
        ),
        out_specs=P(("group", "ctx"), "head"),
        check_vma=False,
    )
```

profile of v0, /device:TPU:0, one launch (start us, length us, event | category | flops | bytes accessed | tf_op | source)
XLA Modules:
  0.0 54.3 jit_solution(1356977436039085521)
XLA Ops:
  0.0 0.0 copy-start
  0.0 0.9 %dynamic_slice.12 = f32[128]{0:T(128)S(1)} dynamic-slice(f32[512]{0:T(512)} %param.12, s32[]{:T(128)S(6)} %select_n.69), dynamic_slice_sizes={128} | dynamic-slice | bytes 1028 | tf_op jit(solution)/shard_map/dynamic_slice | solution.py:115
  0.9 0.8 %fusion.33 = f32[64]{0:T(128)S(1)} fusion(bf16[64,128]{1,0:T(8,128)(2,1)} %param.10), kind=kLoop, calls=%fused_computation.34 | loop fusion | flops 24512 | bytes 16640 | tf_op jit(solution)/shard_map/reduce_sum | solution.py:114
  1.7 8.4 %psum.7 = f32[64]{0:T(128)S(1)} all-reduce(f32[64]{0:T(128)S(1)} %fusion.33), channel_id=1, replica_groups=mesh['group'=2,'ctx'=4,'head'=4] {'head'}, use_global_device_ids=true, to_apply=%region_3.4 | all-reduce | flops 64 | bytes 512 | tf_op jit(solution)/shard_map/psum | solution.py:114
  10.1 0.8 %fusion.35 = bf16[64,128]{1,0:T(8,128)(2,1)S(1)} fusion(bf16[64,128]{1,0:T(8,128)(2,1)} %param.10, f32[128]{0:T(128)S(1)} %dynamic_slice.12, f32[64]{0:T(128)S(1)} %add_rsqrt_fusion), kind=kLoop, calls=%fused_computation.36 | loop fusion | flops 32768 | bytes 33536 | tf_op jit(solution)/shard_map/convert_element_type | solution.py:118
  10.9 5.3 %all_gather.9 = bf16[64,512]{1,0:T(8,128)(2,1)S(1)} all-gather(bf16[64,128]{1,0:T(8,128)(2,1)S(1)} %fusion.35), channel_id=1, replica_groups=mesh['group'=2,'ctx'=4,'head'=4] {'head'}, dimensions={1}, use_global_device_ids=true | all-gather | bytes 81920 | tf_op jit(solution)/shard_map/all_gather | solution.py:119
  16.2 14.1 %all_gather.10 = bf16[256,512]{1,0:T(8,128)(2,1)S(1)} all-gather(bf16[64,512]{1,0:T(8,128)(2,1)S(1)} %all_gather.9), channel_id=1, replica_groups=mesh['group'=2,'ctx'=4,'head'=4] {'ctx'}, dimensions={0}, use_global_device_ids=true | all-gather | bytes 327680 | tf_op jit(solution)/shard_map/all_gather | solution.py:121
  30.2 0.0 copy-done
  30.2 1.8 %fusion.9 = bf16[64,16,512]{2,0,1:T(8,128)(2,1)S(1)} fusion(bf16[512,2048]{1,0:T(8,128)(2,1)S(1)} %copy-done, bf16[64,2048]{1,0:T(8,128)(2,1)} %param.8), kind=kOutput, calls=%fused_computation.8 | convolution fusion | flops 134742016 | bytes 3407872 | tf_op jit(solution)/shard_map/thd,lhd->thl/dot_general | solution.py:93
  32.0 0.0 copy-start.3
  32.1 0.0 copy-start.2
  32.1 0.0 copy-start.1
  32.1 0.6 %copy.21 = bf16[64,16,512]{2,1,0:T(8,128)(2,1)S(1)} copy(bf16[64,16,512]{2,0,1:T(8,128)(2,1)S(1)} %fusion.9) | data formatting | bytes 2097152 | tf_op jit(solution)/shard_map/convert_element_type | solution.py:99
  32.7 1.5 %fusion.46 = f32[1024,256]{0,1:T(8,128)} fusion(bf16[1024,512]{1,0:T(8,128)(2,1)S(1)} %bitcast.45, bf16[256,512]{1,0:T(8,128)(2,1)S(1)} %all_gather.10), kind=kOutput, calls=%fused_computation.68 | convolution fusion | flops 268435456 | bytes 2359296 | tf_op jit(solution)/shard_map/while/body/eval_jaxpr/dot_general | solution.py:60
  34.1 0.0 copy-done.3
  34.2 0.1 select_reduce_fusion.1
  34.3 0.0 copy-done.2
  34.3 0.2 multiply_cosine_fusion
  34.5 0.1 pad_maximum_fusion
  34.6 13.3 %all_gather.11 = bf16[256,64]{1,0:T(8,128)(2,1)S(1)} all-gather(bf16[64,64]{1,0:T(8,128)(2,1)S(1)} %pad_maximum_fusion), channel_id=1, replica_groups=mesh['group'=2,'ctx'=4,'head'=4] {'ctx'}, dimensions={0}, use_global_device_ids=true | all-gather | bytes 40960 | tf_op jit(solution)/shard_map/all_gather | solution.py:122
  47.9 0.0 copy-done.1
  47.9 0.1 reshape.178
  48.0 0.2 subtract_convert_fusion
  48.2 0.1 broadcast_in_dim.74
  48.3 0.1 le.23
  48.4 0.1 select_reduce_fusion
  48.5 1.7 %fusion.45 = (f32[1024]{0:T(1024)S(1)}, f32[1024,256]{0,1:T(8,128)S(1)}) fusion(f32[1024,256]{0,1:T(8,128)} %fusion.46, bf16[256,64]{1,0:T(8,128)(2,1)S(1)} %all_gather.11, bf16[1024,32]{1,0:T(8,128)(2,1)S(1)} %bitcast.47, bf16[1024,32]{1,0:T(8,128)(2,1)S(1)} %bitcast.46, s32[1024]{0:T(1024)S(1)} %le.23, s32[256]{0:T(256)S(1)} %fusion.38), kind=kOutput, calls=%fused_computation.67 | convolution fusion | flops 35126272 | bytes 2270208 | tf_op jit(solution)/shard_map/while/body/eval_jaxpr/dot_general | solution.py:63
  50.2 0.2 fusion.21
  50.4 0.0 copy-start.4
  50.4 0.6 %divide_convert_fusion = bf16[1024,512]{1,0:T(8,128)(2,1)S(1)} fusion(bf16[256,512]{1,0:T(8,128)(2,1)S(1)} %all_gather.10, f32[1024]{0:T(1024)S(1)} %get-tuple-element.40, f32[1024]{0:T(1024)S(1)} %get-tuple-element.29, f32[1024,256]{0,1:T(8,128)S(1)} %get-tuple-element.48, f32[1024]{0:T(1024)S(1)} %broadcast_maximum_fusion, s32[1024]{0:T(1024)S(1)} %le.23, ...), kind=kOutput, calls=%fused_computation.6 | convolution fusion | flops 271056896 | bytes 2376704 | tf_op jit(solution)/shard_map/while/body/eval_jaxpr/dot_general | solution.py:71
  51.0 1.0 %copy-done.4 = bf16[512,2048]{1,0:T(8,128)(2,1)S(1)} copy-done((bf16[512,2048]{1,0:T(8,128)(2,1)S(1)}, bf16[512,2048]{1,0:T(8,128)(2,1)}, u32[]{:S(2)}) %copy-start.4) | copy-done | bytes 2097176
  52.0 1.5 %fusion.17 = bf16[16,8,8,128]{3,2,1,0:T(8,128)(2,1)S(1)} fusion(bf16[64,16,512]{2,1,0:T(8,128)(2,1)S(1)} %bitcast.48, bf16[512,2048]{1,0:T(8,128)(2,1)S(1)} %copy-done.4), kind=kOutput, calls=%fused_computation.14 | convolution fusion | flops 134348800 | bytes 3407872 | tf_op jit(solution)/shard_map/thl,lhe->the/dot_general | solution.py:157
  53.5 0.8 %copy.52 = bf16[16,8,8,128]{3,2,0,1:T(8,128)(2,1)} copy(bf16[16,8,8,128]{3,2,1,0:T(8,128)(2,1)S(1)} %fusion.17) | data formatting | bytes 524288 | tf_op jit(solution)/shard_map/reshape | solution.py:163
  (9 shorter events, 0.1 us)
Async XLA Ops:
  0.0 30.2 %copy-start = (bf16[512,2048]{1,0:T(8,128)(2,1)S(1)}, bf16[512,2048]{1,0:T(8,128)(2,1)}, u32[]{:S(2)}) copy-start(bf16[512,2048]{1,0:T(8,128)(2,1)} %param.13) | copy-start | bytes 6291460
  32.0 2.1 %copy-start.3 = (s32[8]{0:T(128)S(1)}, s32[8]{0:T(128)}, u32[]{:S(2)}) copy-start(s32[8]{0:T(128)} %param.15) | copy-start | bytes 100
  32.1 2.2 %copy-start.2 = (bf16[64,64]{1,0:T(8,128)(2,1)S(1)}, bf16[64,64]{1,0:T(8,128)(2,1)}, u32[]{:S(2)}) copy-start(bf16[64,64]{1,0:T(8,128)(2,1)} %param.11) | copy-start | bytes 24580
  32.1 15.8 %copy-start.1 = (bf16[64,1024]{1,0:T(8,128)(2,1)S(1)}, bf16[64,1024]{1,0:T(8,128)(2,1)}, u32[]{:S(2)}) copy-start(bf16[64,1024]{1,0:T(8,128)(2,1)} %param.9) | copy-start | bytes 393220
  50.4 1.6 %copy-start.4 = (bf16[512,2048]{1,0:T(8,128)(2,1)S(1)}, bf16[512,2048]{1,0:T(8,128)(2,1)}, u32[]{:S(2)}) copy-start(bf16[512,2048]{1,0:T(8,128)(2,1)} %param.14) | copy-start | bytes 6291460
where the time goes:
time: 54.7 us; the launch traced here: 54.3 us
  blocking collectives  41 us (75%)
  matrix products  7 us (13%)
  local copies, waits for them, and re-layouts  3.53 us (6%)
  other arithmetic  2.6 us (5%)
    all_gather x1, blocking collectives, per_device(): key_latent = lax.all_gather(normed, 'ctx', axis=0, tiled=True)  14.1 us
    all_gather x1, blocking collectives, per_device(): make_key_rotated = lax.all_gather(key_rotated, 'ctx', axis=0, tiled=True)  13.3 us
    psum x1, blocking collectives, per_device(): square = lax.psum(jnp.sum(column_part * column_part, axis=1), 'head')  8.37 us
    all_gather x1, blocking collectives, per_device(): normed = lax.all_gather(scaled, 'head', axis=1, tiled=True)  5.25 us
    dot_general x1, matrix products, per_device(): jnp.einsum('thd,lhd->thl', query_nope.reshape(tokens_here, heads_here, NO...  1.79 us
    dot_general x1, matrix products, attend_block(): lax.dot_general(query_rotated, key_rotated, contract, preferred_element_t...  1.65 us
    dot_general x1, matrix products, per_device(): jnp.einsum('thl,lhe->the', mixed, w_value.reshape(latent_width, heads_her...  1.49 us
    dot_general x1, matrix products, attend_block(): lax.dot_general(query_latent, key_latent, contract, preferred_element_typ...  1.46 us

commit v1 on v0

--- a/solution.py
+++ b/solution.py
@@ -118,8 +118,9 @@
     ).astype(jnp.bfloat16)
     normed = lax.all_gather(scaled, "head", axis=1, tiled=True)
     key_rotated = rotate_pairs(key_rope.astype(jnp.float32), query_angle).astype(jnp.bfloat16)
-    key_latent = lax.all_gather(normed, "ctx", axis=0, tiled=True)
-    make_key_rotated = lax.all_gather(key_rotated, "ctx", axis=0, tiled=True)
+    d_next = jnp.concatenate([normed, key_rotated], axis=1)
+    spare = lax.all_gather(d_next, axis_name="ctx", axis=0, tiled=True)
+    key_latent, make_key_rotated = jnp.split(spare, [normed.shape[1]], axis=1)
     row_count = key_latent.shape[0]
     length = block_length(row_count, tokens_here)
     block_count = row_count // length

time: 54.7 us -> 43.2 us (0.79)
  blocking collectives: 41 us -> 28.1 us
  other arithmetic: 2.6 us -> 3.98 us
    all_gather x2 -> x1, blocking collectives: 27.4 us -> 14.5 us  [per_device(): spare = lax.all_gather(d_next, axis_name='ctx', axis=0, tiled=True)]
    convert_element_type x1, other arithmetic: 0.01 us -> 0.72 us  [per_device(): key_rope.astype(jnp.float32)]
    reduce_sum x2, other arithmetic: 0.17 us -> 0.82 us  [block_positions(): jnp.sum(jnp.where(blocks[:, None] == slot_ids[None, :], table[None, :], 0...]
where the time goes in v1:
time: 43.2 us; the launch traced here: 42.7 us
  blocking collectives  28.1 us (65%)
  matrix products  7.02 us (16%)
  other arithmetic  3.98 us (9%)
  local copies, waits for them, and re-layouts  3.51 us (8%)
    all_gather x1, blocking collectives, per_device(): spare = lax.all_gather(d_next, axis_name='ctx', axis=0, tiled=True)  14.5 us
    psum x1, blocking collectives, per_device(): square = lax.psum(jnp.sum(column_part * column_part, axis=1), 'head')  8.37 us
    all_gather x1, blocking collectives, per_device(): normed = lax.all_gather(scaled, 'head', axis=1, tiled=True)  5.25 us
    dot_general x1, matrix products, per_device(): jnp.einsum('thd,lhd->thl', query_nope.reshape(tokens_here, heads_here, NO...  1.79 us
    dot_general x1, matrix products, attend_block(): lax.dot_general(query_rotated, key_rotated, contract, preferred_element_t...  1.65 us
    dot_general x1, matrix products, per_device(): jnp.einsum('thl,lhe->the', mixed, w_value.reshape(latent_width, heads_her...  1.49 us
    dot_general x1, matrix products, attend_block(): lax.dot_general(query_latent, key_latent, contract, preferred_element_typ...  1.46 us
    unnamed x8, local copies, waits for them, and re-layouts  0.97 us

profile of v1, /device:TPU:0, one launch (start us, length us, event | category | flops | bytes accessed | tf_op | source)
XLA Modules:
  0.0 42.7 jit_solution(16274263337563931323)
XLA Ops:
  0.0 0.0 copy-start
  0.0 0.9 %dynamic_slice.12 = f32[128]{0:T(128)S(1)} dynamic-slice(f32[512]{0:T(512)} %param.12, s32[]{:T(128)S(6)} %select_n.69), dynamic_slice_sizes={128} | dynamic-slice | bytes 1028 | tf_op jit(solution)/shard_map/dynamic_slice | solution.py:115
  0.9 0.8 %fusion.37 = f32[64]{0:T(128)S(1)} fusion(bf16[64,128]{1,0:T(8,128)(2,1)} %param.10), kind=kLoop, calls=%fused_computation.39 | loop fusion | flops 24512 | bytes 16640 | tf_op jit(solution)/shard_map/reduce_sum | solution.py:114
  1.7 8.4 %psum.7 = f32[64]{0:T(128)S(1)} all-reduce(f32[64]{0:T(128)S(1)} %fusion.37), channel_id=1, replica_groups=mesh['group'=2,'ctx'=4,'head'=4] {'head'}, use_global_device_ids=true, to_apply=%region_3.4 | all-reduce | flops 64 | bytes 512 | tf_op jit(solution)/shard_map/psum | solution.py:114
  10.1 0.8 %fusion.39 = bf16[64,128]{1,0:T(8,128)(2,1)S(1)} fusion(bf16[64,128]{1,0:T(8,128)(2,1)} %param.10, f32[128]{0:T(128)S(1)} %dynamic_slice.12, f32[64]{0:T(128)S(1)} %add_rsqrt_fusion), kind=kLoop, calls=%fused_computation.41 | loop fusion | flops 32768 | bytes 33536 | tf_op jit(solution)/shard_map/convert_element_type | solution.py:118
  10.9 5.3 %all_gather.6 = bf16[64,512]{1,0:T(8,128)(2,1)S(1)} all-gather(bf16[64,128]{1,0:T(8,128)(2,1)S(1)} %fusion.39), channel_id=1, replica_groups=mesh['group'=2,'ctx'=4,'head'=4] {'head'}, dimensions={1}, use_global_device_ids=true | all-gather | bytes 81920 | tf_op jit(solution)/shard_map/all_gather | solution.py:119
  16.2 0.7 %select_reduce_fusion.1 = s32[64]{0:T(128)S(1)} fusion(s32[8]{0:T(128)} %param.15, s32[64]{0:T(128)S(1)} %and_select_fusion.1), kind=kLoop, calls=%fused_computation.47 | loop fusion | flops 1472 | bytes 544 | tf_op jit(solution)/shard_map/reduce_sum | solution.py:36
  16.9 0.7 %convert_element_type.43 = f32[64,64]{1,0:T(8,128)S(1)} convert(bf16[64,64]{1,0:T(8,128)(2,1)} %param.11) | non-fusion elementwise | flops 4096 | bytes 24576 | tf_op jit(solution)/shard_map/convert_element_type | solution.py:120
  17.7 0.2 multiply_cosine_fusion
  17.9 0.1 pad_maximum_fusion
  17.9 14.5 %all_gather.7 = bf16[256,576]{1,0:T(8,128)(2,1)S(1)} all-gather(bf16[64,576]{1,0:T(8,128)(2,1)S(1)} %pad_maximum_fusion), channel_id=1, replica_groups=mesh['group'=2,'ctx'=4,'head'=4] {'ctx'}, dimensions={0}, use_global_device_ids=true | all-gather | bytes 368640 | tf_op jit(solution)/shard_map/all_gather | solution.py:122
  32.4 0.0 copy-done
  32.4 1.8 %fusion.9 = bf16[64,16,512]{2,0,1:T(8,128)(2,1)S(1)} fusion(bf16[512,2048]{1,0:T(8,128)(2,1)S(1)} %copy-done, bf16[64,2048]{1,0:T(8,128)(2,1)} %param.8), kind=kOutput, calls=%fused_computation.8 | convolution fusion | flops 134742016 | bytes 3407872 | tf_op jit(solution)/shard_map/thd,lhd->thl/dot_general | solution.py:93
  34.2 0.0 copy-start.1
  34.2 0.6 %copy.21 = bf16[64,16,512]{2,1,0:T(8,128)(2,1)S(1)} copy(bf16[64,16,512]{2,0,1:T(8,128)(2,1)S(1)} %fusion.9) | data formatting | bytes 2097152 | tf_op jit(solution)/shard_map/convert_element_type | solution.py:99
  34.8 0.0 copy-start.2
  34.8 1.5 %fusion.34 = f32[1024,256]{0,1:T(8,128)} fusion(bf16[1024,512]{1,0:T(8,128)(2,1)S(1)} %bitcast.42, bf16[256,576]{1,0:T(8,128)(2,1)S(1)} %all_gather.7), kind=kOutput, calls=%fused_computation.31 | convolution fusion | flops 268435456 | bytes 2359296 | tf_op jit(solution)/shard_map/while/body/eval_jaxpr/dot_general | solution.py:60
  36.3 0.0 copy-done.1
  36.3 0.1 reshape.178
  36.5 0.2 subtract_convert_fusion
  36.7 0.1 broadcast_in_dim.74
  36.8 0.1 le.23
  36.8 0.0 copy-done.2
  36.9 0.1 select_reduce_fusion
  36.9 1.6 %fusion.49 = (f32[1024]{0:T(1024)S(1)}, f32[1024,256]{0,1:T(8,128)S(1)}) fusion(f32[1024,256]{0,1:T(8,128)} %fusion.34, bf16[256,576]{1,0:T(8,128)(2,1)S(1)} %all_gather.7, bf16[1024,32]{1,0:T(8,128)(2,1)S(1)} %bitcast.44, bf16[1024,32]{1,0:T(8,128)(2,1)S(1)} %bitcast.43, s32[1024]{0:T(1024)S(1)} %le.23, s32[256]{0:T(256)S(1)} %fusion.42), kind=kOutput, calls=%fused_computation.71 | convolution fusion | flops 35126272 | bytes 2696192 | tf_op jit(solution)/shard_map/while/body/eval_jaxpr/dot_general | solution.py:63
  38.6 0.2 fusion.21
  38.9 0.0 copy-start.3
  38.9 0.6 %divide_convert_fusion = bf16[1024,512]{1,0:T(8,128)(2,1)S(1)} fusion(f32[1024]{0:T(1024)S(1)} %get-tuple-element.40, f32[1024]{0:T(1024)S(1)} %get-tuple-element.29, f32[1024,256]{0,1:T(8,128)S(1)} %get-tuple-element.48, f32[1024]{0:T(1024)S(1)} %broadcast_maximum_fusion, s32[1024]{0:T(1024)S(1)} %le.23, s32[256]{0:T(256)S(1)} %fusion.42, ...), kind=kOutput, calls=%fused_computation.6 | convolution fusion | flops 271056896 | bytes 2376704 | tf_op jit(solution)/shard_map/while/body/eval_jaxpr/dot_general | solution.py:71
  39.5 1.0 %copy-done.3 = bf16[512,2048]{1,0:T(8,128)(2,1)S(1)} copy-done((bf16[512,2048]{1,0:T(8,128)(2,1)S(1)}, bf16[512,2048]{1,0:T(8,128)(2,1)}, u32[]{:S(2)}) %copy-start.3) | copy-done | bytes 2097176
  40.5 1.5 %fusion.17 = bf16[16,8,8,128]{3,2,1,0:T(8,128)(2,1)S(1)} fusion(bf16[64,16,512]{2,1,0:T(8,128)(2,1)S(1)} %bitcast.45, bf16[512,2048]{1,0:T(8,128)(2,1)S(1)} %copy-done.3), kind=kOutput, calls=%fused_computation.14 | convolution fusion | flops 134348800 | bytes 3407872 | tf_op jit(solution)/shard_map/thl,lhe->the/dot_general | solution.py:158
  42.0 0.8 %copy.52 = bf16[16,8,8,128]{3,2,0,1:T(8,128)(2,1)} copy(bf16[16,8,8,128]{3,2,1,0:T(8,128)(2,1)S(1)} %fusion.17) | data formatting | bytes 524288 | tf_op jit(solution)/shard_map/reshape | solution.py:164
  (8 shorter events, 0.1 us)
Async XLA Ops:
  0.0 32.4 %copy-start = (bf16[512,2048]{1,0:T(8,128)(2,1)S(1)}, bf16[512,2048]{1,0:T(8,128)(2,1)}, u32[]{:S(2)}) copy-start(bf16[512,2048]{1,0:T(8,128)(2,1)} %param.13) | copy-start | bytes 6291460
  34.2 2.1 %copy-start.1 = (bf16[64,1024]{1,0:T(8,128)(2,1)S(1)}, bf16[64,1024]{1,0:T(8,128)(2,1)}, u32[]{:S(2)}) copy-start(bf16[64,1024]{1,0:T(8,128)(2,1)} %param.9) | copy-start | bytes 393220
  34.8 2.0 %copy-start.2 = (s32[8]{0:T(128)S(1)}, s32[8]{0:T(128)}, u32[]{:S(2)}) copy-start(s32[8]{0:T(128)} %param.15) | copy-start | bytes 100
  38.9 1.6 %copy-start.3 = (bf16[512,2048]{1,0:T(8,128)(2,1)S(1)}, bf16[512,2048]{1,0:T(8,128)(2,1)}, u32[]{:S(2)}) copy-start(bf16[512,2048]{1,0:T(8,128)(2,1)} %param.14) | copy-start | bytes 6291460
